TPU v7x, 32 devices: a whole 2x2x4 slice. The times are simulated.
32 devices in a mesh: lat: 4 (over z), lon: 8 (over y, x, core).
Axes of the slice: x: 2, y: 2, z: 4, core: 2. Of those that a mesh axis runs over, the one named last changes fastest.
Arguments:
- zonal_wind: float32 [32, 32, 2048], P(None, 'lat', 'lon'), may hold values from -6 to 6
- merid_wind: float32 [32, 32, 2048], P(None, 'lat', 'lon'), may hold values from -6 to 6
- vertical_wind: float32 [32, 32, 2048], P(None, 'lat', 'lon'), may hold values from -6 to 6
- pressure: float32 [32, 32, 2048], P(None, 'lat', 'lon'), may hold values from -6 to 6
- zonal_coef: float32 [32], P('lat'), may hold values from 0.05 to 0.4
- merid_coef: float32 [32], P('lat'), may hold values from 0.05 to 0.4
- level_coef: float32 [32], replicated, may hold values from 0.3 to 1.5
- sound_coef: float32 [32, 32, 2048], P(None, 'lat', 'lon'), may hold values from 0.2 to 2
- cutoff: int32 [32], replicated, may hold values from 1 to 511
- filter_mask: int32 [32], replicated, may hold values from 0 to 1, as said below
Outputs:
- zonal_next: float32 [32, 32, 2048], P(None, 'lat', 'lon')
- merid_next: float32 [32, 32, 2048], P(None, 'lat', 'lon')
- vertical_next: float32 [32, 32, 2048], P(None, 'lat', 'lon')
- pressure_next: float32 [32, 32, 2048], P(None, 'lat', 'lon')
Inputs may be any that keep to these rules, and one draw needn't show every extreme that they name: `filter_mask`: for every latitude j below 16 exactly one of j and j + 16 is filtered; the filtered ones are the first n and the last 16 - n latitudes, for some n from 4 to 12.
All inputs are finite; a program needn't handle non-finite values.
Results may differ from a plain program's by a relative error of at most 0.0001.
Values sent between devices are 32-bit elements; how exact they have to be, the bound alone decides.
No kernel may reach another device: no remote copies, remote signals or barrier semaphores. Data moves between devices by JAX's collectives and lax.ppermute only.
A program may use at most 64 MiB of HBM per device.

v0:
```python
import math
import jax
import jax.numpy as jnp
from jax import lax
from jax.sharding import PartitionSpec as P

SUBSTEPS = 2


def extended(block, sides, width):
    for axis, dim in sides:
        count = lax.axis_size(axis)
        forward = [(i, i + 1) for i in range(count - 1)]
        forward.append((count - 1, 0))
        backward = [(target, source) for source, target in forward]
        low = lax.ppermute(
            lax.slice_in_dim(block, block.shape[dim] - width, None, axis=dim), axis, forward
        )
        high = lax.ppermute(lax.slice_in_dim(block, 0, width, axis=dim), axis, backward)
        block = jnp.concatenate([low, block, high], axis=dim)
    return block


def rim_fix(padded, lat_dim):
    band_index = lax.axis_index("lat")
    bands = lax.axis_size("lat")
    extent = padded.shape[lat_dim]
    position = lax.broadcasted_iota(jnp.int32, padded.shape, lat_dim)
    first_edge = jnp.logical_and(position == 0, band_index == 0)
    final_edge = jnp.logical_and(position == extent - 1, band_index == bands - 1)
    return jnp.where(jnp.logical_or(first_edge, final_edge), 0.0, padded)


def dft_tables(length):
    half_len = length // 2
    sample = lax.broadcasted_iota(jnp.int32, (length, length), 0)
    column = lax.broadcasted_iota(jnp.int32, (length, length), 1)
    is_cosine = column <= half_len
    wavenum = jnp.where(is_cosine, column, column - half_len)
    phase = sample * wavenum % length
    angle = 2.0 * math.pi / length * phase.astype(jnp.float32)
    forward = jnp.where(is_cosine, jnp.cos(angle), jnp.sin(angle))
    single = jnp.logical_and(is_cosine, jnp.logical_or(wavenum == 0, wavenum == half_len))
    weight = jnp.where(single, 1.0, 2.0) / length
    inverse = jnp.transpose(forward * weight)
    wave_row = wavenum[0].astype(jnp.float32)
    return (forward, inverse, wave_row)


def damping(wave_row, limits):
    bound_col = limits[:, None]
    ratio = bound_col / jnp.maximum(wave_row[None, :], 1.0)
    return jnp.where(wave_row[None, :] > bound_col, ratio * ratio, 1.0)


def transform_band(block, limits, forward, inverse, wave_row):
    circles = lax.all_to_all(block, "lon", split_axis=1, concat_axis=3, tiled=True)
    spectra = jnp.einsum("vetj,jc->vetc", circles, forward, precision=lax.Precision.HIGHEST)
    scaled = spectra * damping(wave_row, limits)
    damped = jnp.einsum("vetc,cj->vetj", scaled, inverse, precision=lax.Precision.HIGHEST)
    return lax.all_to_all(damped, "lon", split_axis=3, concat_axis=1, tiled=True)


def filtered_increments(increments, own_flags, own_limits, forward, inverse, wave_row):
    flag_cols = own_flags[:, None]
    damped = transform_band(increments, own_limits, forward, inverse, wave_row)
    return jnp.where(flag_cols, damped, increments)


def column_solve(vertical_wind, pstar, level_coef, sound_coef):
    levels = vertical_wind.shape[0]
    zero_slab = jnp.zeros_like(vertical_wind[0])
    ratios = []
    values = []
    prev_ratio = zero_slab
    prev_value = zero_slab
    for level in range(levels):
        alpha = level_coef[level]
        below = alpha * sound_coef[level]
        if level + 1 < levels:
            above = alpha * sound_coef[level + 1]
            rhs = vertical_wind[level] - alpha * (pstar[level + 1] - pstar[level])
        else:
            above = zero_slab
            rhs = vertical_wind[level] + alpha * pstar[level]
        pivot = 1.0 + below + above + below * prev_ratio
        prev_ratio = -above / pivot
        prev_value = (rhs + below * prev_value) / pivot
        ratios.append(prev_ratio)
        values.append(prev_value)
    solved = [zero_slab] * levels
    upper_value = values[levels - 1]
    solved[levels - 1] = upper_value
    for level in range(levels - 2, -1, -1):
        upper_value = values[level] - ratios[level] * upper_value
        solved[level] = upper_value
    new_wind = jnp.stack(solved)
    wind_below = jnp.concatenate([zero_slab[None], new_wind[:-1]], axis=0)
    new_pressure = pstar - sound_coef * (new_wind - wind_below)
    return (new_wind, new_pressure)


def body(
    zonal_wind,
    merid_wind,
    vertical_wind,
    pressure,
    zonal_coef,
    merid_coef,
    level_coef,
    sound_coef,
    cutoff,
    filter_mask,
):
    lat_rows = pressure.shape[1]
    start = lax.axis_index("lat") * lat_rows
    own_flags = lax.dynamic_slice_in_dim(filter_mask, start, lat_rows) > 0
    own_limits = lax.dynamic_slice_in_dim(cutoff, start, lat_rows).astype(jnp.float32)
    forward, inverse, wave_row = dft_tables(pressure.shape[2] * lax.axis_size("lon"))
    zonal_rows = zonal_coef[None, :, None]
    merid_rows = merid_coef[None, :, None]
    for step in range(SUBSTEPS):
        padded = extended(pressure, (("lat", 1), ("lon", 2)), 1)
        padded = rim_fix(padded, 1)
        zonal_step = -zonal_rows * (padded[:, 1:-1, 2:] - padded[:, 1:-1, :-2])
        merid_step = -merid_rows * (padded[:, 2:, 1:-1] - padded[:, :-2, 1:-1])
        increments = jnp.stack([zonal_step, merid_step])
        damped = filtered_increments(increments, own_flags, own_limits, forward, inverse, wave_row)
        winds = jnp.stack([zonal_wind, merid_wind]) + damped
        wind_pad = extended(winds, (("lat", 2), ("lon", 3)), 1)
        wind_pad = rim_fix(wind_pad, 2)
        diverge = zonal_rows * (wind_pad[0, :, 1:-1, 2:] - wind_pad[0, :, 1:-1, :-2])
        diverge = diverge + merid_rows * (wind_pad[1, :, 2:, 1:-1] - wind_pad[1, :, :-2, 1:-1])
        pstar = pressure - sound_coef * diverge
        vertical_wind, pressure = column_solve(vertical_wind, pstar, level_coef, sound_coef)
        zonal_wind = winds[0]
        merid_wind = winds[1]
    return (zonal_wind, merid_wind, vertical_wind, pressure)


def solution(mesh):
    in_specs = (
        P(None, "lat", "lon"),
        P(None, "lat", "lon"),
        P(None, "lat", "lon"),
        P(None, "lat", "lon"),
        P("lat"),
        P("lat"),
        P(),
        P(None, "lat", "lon"),
        P(),
        P(),
    )
    out_specs = (
        P(None, "lat", "lon"),
        P(None, "lat", "lon"),
        P(None, "lat", "lon"),
        P(None, "lat", "lon"),
    )
    return jax.shard_map(body, mesh=mesh, in_specs=in_specs, out_specs=out_specs, check_vma=False)
```

profile of v0, /device:TPU:0, one launch (start us, length us, event | category | flops | bytes accessed | tf_op | source)
XLA Modules:
  0.0 585.0 jit_solution(11969171518378575389)
XLA Ops:
  1.8 5.1 collective-permute-start.1
  9.1 3.5 collective-permute-done
  13.5 6.0 %collective-permute-done.3 = f32[32,10,1]{2,1,0:T(8,128)S(1)} collective-permute-done((f32[32,10,1]{2,1,0:T(8,128)S(1)}, f32[32,10,1]{2,1,0:T(8,128)S(1)}, u32[]{:S(2)}, u32[]{:S(2)}) %collective-permute-start.3) | collective-permute-done | bytes 1312 | tf_op jit(solution)/shard_map/ppermute | solution.py:19
  19.5 3.0 collective-permute-done.2
  24.2 3.8 all-to-all-start
  28.2 9.5 %all-to-all-done = f32[2,32,8,256]{3,2,0,1:T(8,128)S(1)} async-done(((f32[2,32,8,256]{3,2,0,1:T(8,128)}), f32[2,32,8,256]{3,2,0,1:T(8,128)S(1)}, u32[]{:S(2)}, u32[]{:S(2)}) %all-to-all-start) | async-done | bytes 524320 | tf_op jit(solution)/shard_map/all_to_all | solution.py:57
  38.0 75.8 %fusion.15 = f32[2,4,8,2048]{3,2,1,0:T(8,128)S(1)} fusion(f32[2,4,8,2048]{3,2,1,0:T(8,128)S(1)} %all_to_all.55, s32[2048]{0:T(1024)S(1)} %iota_add_fusion, pred[2048]{0:T(1024)(128)(4,1)S(1)} %iota_compare_fusion, f32[8,2048]{1,0:T(8,128)S(1)} %fusion.44), kind=kOutput, calls=%fused_computation.21 | convolution fusion | flops 3288465408 | bytes 1124352 | tf_op jit(solution)/shard_map/vetj,jc->vetc/dot_general | solution.py:58
  113.9 82.4 %fusion.5 = f32[2,4,8,2048]{3,2,1,0:T(8,128)S(1)} fusion(f32[2,4,8,2048]{3,2,1,0:T(8,128)S(1)} %fusion.15, s32[2048]{0:T(1024)S(1)} %iota_add_fusion, pred[2048]{0:T(1024)(128)(4,1)S(1)} %iota_compare_fusion), kind=kOutput, calls=%fused_computation.8 | convolution fusion | flops 3317694464 | bytes 1058816 | tf_op jit(solution)/shard_map/vetc,cj->vetj/dot_general | solution.py:60
  196.4 5.8 copy.23
  202.1 12.3 %reshape.77 = f32[8,1,16384]{2,1,0:T(1,128)} reshape(f32[2048,2,4,8]{3,2,1,0:T(4,128)} %bitcast.161) | data formatting | bytes 1048576
  214.4 3.6 all-to-all-start.1
  218.1 9.6 %all-to-all-done.1 = f32[8,1,16384]{2,1,0:T(1,128)S(1)} async-done(((f32[8,1,16384]{2,1,0:T(1,128)}), f32[8,1,16384]{2,1,0:T(1,128)S(1)}, u32[]{:S(2)}, u32[]{:S(2)}) %all-to-all-start.1) | async-done | bytes 524320 | tf_op jit(solution)/shard_map/all_to_all | solution.py:61
  230.1 13.2 %reshape.78 = f32[2048,2,4,8]{3,2,1,0:T(4,128)} reshape(f32[8,16384]{1,0:T(8,128)S(1)} %reduce) | data formatting | bytes 1048576
  243.3 6.7 %copy.24 = f32[2,4,8,8,256]{4,2,0,1,3:T(8,128)S(1)} copy(f32[2,4,8,8,256]{2,1,0,4,3:T(4,128)} %bitcast.162) | data formatting | bytes 1048576 | tf_op jit(solution)/shard_map/all_to_all | solution.py:61
  254.5 2.1 collective-permute-done.4
  258.8 10.3 %collective-permute-done.7 = f32[2,32,10,1]{3,2,1,0:T(8,128)S(1)} collective-permute-done((f32[2,32,10,1]{3,2,1,0:T(8,128)S(1)}, f32[2,32,10,1]{3,2,1,0:T(8,128)S(1)}, u32[]{:S(2)}, u32[]{:S(2)}) %collective-permute-start.7) | collective-permute-done | bytes 2592 | tf_op jit(solution)/shard_map/ppermute | solution.py:19
  272.0 20.4 %add_divide_fusion.32 = (f32[1,8,256]{2,1,0:T(8,128)S(1)}, f32[1,8,256]{2,1,0:T(8,128)S(1)}, f32[1,8,256]{2,1,0:T(8,128)S(1)}, f32[1,8,256]{2,1,0:T(8,128)S(1)},...) fusion(f32[32,8,256]{2,1,0:T(8,128)S(1)} %copy-done.6, ...), kind=kLoop, calls=%fused_computation.313 | loop fusion | flops 882688 | bytes 1523836 | tf_op jit(solution)/shard_map/div | solution.py:88
  297.2 2.2 collective-permute-done.9
  302.0 5.6 collective-permute-done.11
  307.6 2.2 collective-permute-done.10
  311.4 12.3 %all_to_all.72 = f32[2,32,8,256]{3,2,0,1:T(8,128)S(1)} all-to-all(f32[2,32,8,256]{3,2,0,1:T(8,128)S(1)} %copy.29), channel_id=1, replica_groups=mesh['lat'=4,'lon'=8] {'lon'}, dimensions={1} | all-to-all | bytes 1048576 | tf_op jit(solution)/shard_map/all_to_all | solution.py:57
  325.0 77.2 %fusion.18 = f32[2,4,8,2048]{3,2,1,0:T(8,128)S(1)} fusion(f32[2,4,8,2048]{3,2,1,0:T(8,128)} %all_to_all.63, s32[2048]{0:T(1024)} %copy-done.21, pred[2048]{0:T(1024)(128)(4,1)} %copy-done.24, f32[8,2048]{1,0:T(8,128)} %copy-done.20), kind=kOutput, calls=%fused_computation.22 | convolution fusion | flops 3288465408 | bytes 1124352 | tf_op jit(solution)/shard_map/vetj,jc->vetc/dot_general | solution.py:58
  402.2 82.1 %fusion.3 = f32[2,4,8,2048]{3,2,1,0:T(8,128)S(1)} fusion(f32[2,4,8,2048]{3,2,1,0:T(8,128)S(1)} %fusion.18, s32[2048]{0:T(1024)S(1)} %copy-done.22, pred[2048]{0:T(1024)(128)(4,1)S(1)} %copy-done.25), kind=kOutput, calls=%fused_computation.6 | convolution fusion | flops 3317694464 | bytes 1058816 | tf_op jit(solution)/shard_map/vetc,cj->vetj/dot_general | solution.py:60
  484.3 5.8 copy.31
  490.1 11.6 %reshape.79 = f32[8,1,16384]{2,1,0:T(1,128)S(1)} reshape(f32[2048,2,4,8]{3,2,1,0:T(4,128)} %bitcast.163) | data formatting | bytes 1048576
  501.7 12.8 %all_to_all.73 = f32[8,1,16384]{2,1,0:T(1,128)} all-to-all(f32[8,1,16384]{2,1,0:T(1,128)S(1)} %reshape.79), channel_id=1, replica_groups=mesh['lat'=4,'lon'=8] {'lon'}, dimensions={0} | all-to-all | bytes 1048576 | tf_op jit(solution)/shard_map/all_to_all | solution.py:61
  514.5 2.9 reduce.1
  517.4 13.2 %reshape.80 = f32[2048,2,4,8]{3,2,1,0:T(4,128)} reshape(f32[8,16384]{1,0:T(8,128)S(1)} %reduce.1) | data formatting | bytes 1048576
  530.7 6.7 %copy.32 = f32[2,4,8,8,256]{4,2,1,3,0:T(8,128)S(1)} copy(f32[2,4,8,8,256]{2,1,0,4,3:T(4,128)} %bitcast.164) | data formatting | bytes 1048576 | tf_op jit(solution)/shard_map/all_to_all | solution.py:61
  540.5 2.9 collective-permute-done.13
  546.8 10.5 %collective-permute-done.15 = f32[2,32,10,1]{3,2,0,1:T(8,128)S(1)} collective-permute-done((f32[2,32,10,1]{3,2,0,1:T(8,128)S(1)}, f32[2,32,10,1]{3,2,0,1:T(8,128)S(1)}, u32[]{:S(2)}, u32[]{:S(2)}) %collective-permute-start.15) | collective-permute-done | bytes 2592 | tf_op jit(solution)/shard_map/ppermute | solution.py:19
  561.3 20.7 %add_divide_fusion.1 = (f32[1,8,256]{2,1,0:T(8,128)S(1)}, f32[1,8,256]{2,1,0:T(8,128)S(1)}, f32[1,8,256]{2,1,0:T(8,128)S(1)}, f32[1,8,256]{2,1,0:T(8,128)S(1)}, ...) fusion(f32[1,8,256]{2,1,0:T(8,128)S(1)} %get-tuple-element.102,, ...), kind=kLoop, calls=%fused_computation.248 | loop fusion | flops 452608 | bytes 1269884 | tf_op jit(solution)/shard_map/div | solution.py:88
  (199 shorter events, 41.2 us)
Async XLA Ops:
  1.8 7.3 %collective-permute-start.1 = (f32[32,1,256]{2,1,0:T(1,128)S(1)}, f32[32,1,256]{2,1,0:T(1,128)S(1)}, u32[]{:S(2)}, u32[]{:S(2)}) collective-permute-start(f32[32,1,256]{2,1,0:T(1,128)S(1)} %get-tuple-element.213), channel_id=1, source_target_pairs={{8,0},{16,8},{24,16},{0,24},{9,1},{17,9},{25,17},{1,25},{10,2},{18... | collective-permute-start | bytes 98312 | tf_op jit(solution)/shard_map/ppermute | solution.py:19
  6.9 5.7 collective-permute-start
  6.9 106.9 %copy-start.21 = (s32[2048]{0:T(1024)}, s32[2048]{0:T(1024)S(1)}, u32[]{:S(2)}) copy-start(s32[2048]{0:T(1024)S(1)} %iota_add_fusion) | copy-start | bytes 24580
  6.9 106.9 %copy-start.24 = (pred[2048]{0:T(1024)(128)(4,1)}, pred[2048]{0:T(1024)(128)(4,1)S(1)}, u32[]{:S(2)}) copy-start(pred[2048]{0:T(1024)(128)(4,1)S(1)} %iota_compare_fusion) | copy-start | bytes 6148
  12.9 6.7 %collective-permute-start.3 = (f32[32,10,1]{2,1,0:T(8,128)S(1)}, f32[32,10,1]{2,1,0:T(8,128)S(1)}, u32[]{:S(2)}, u32[]{:S(2)}) collective-permute-start(f32[32,10,1]{2,1,0:T(8,128)S(1)} %get-tuple-element.209), channel_id=1, source_target_pairs={{1,0},{2,1},{3,2},{4,3},{5,4},{6,5},{7,6},{0,7},{9,8},{10,9},{11,1... | collective-permute-start | bytes 3848 | tf_op jit(solution)/shard_map/ppermute | solution.py:19
  13.4 9.2 %collective-permute-start.2 = (f32[32,10,1]{2,1,0:T(8,128)S(1)}, f32[32,10,1]{2,1,0:T(8,128)S(1)}, u32[]{:S(2)}, u32[]{:S(2)}) collective-permute-start(f32[32,10,1]{2,1,0:T(8,128)S(1)} %get-tuple-element.208), channel_id=1, source_target_pairs={{0,1},{1,2},{2,3},{3,4},{4,5},{5,6},{6,7},{7,0},{8,9},{9,10},{10,1... | collective-permute-start | bytes 3848 | tf_op jit(solution)/shard_map/ppermute | solution.py:16
  13.4 296.4 %copy-start.26 = (pred[10]{0:T(512)(128)(4,1)}, pred[10]{0:T(512)(128)(4,1)S(1)}, u32[]{:S(2)}) copy-start(pred[10]{0:T(512)(128)(4,1)S(1)} %and_or_fusion) | copy-start | bytes 34
  13.5 100.4 %copy-start.29 = (f32[8]{0:T(128)}, f32[8]{0:T(128)S(1)}, u32[]{:S(2)}) copy-start(f32[8]{0:T(128)S(1)} %neg.2118) | copy-start | bytes 100
  13.5 100.4 %copy-start.30 = (f32[8]{0:T(128)}, f32[8]{0:T(128)S(1)}, u32[]{:S(2)}) copy-start(f32[8]{0:T(128)S(1)} %neg.2119) | copy-start | bytes 100
  24.2 13.4 %all-to-all-start = ((f32[2,32,8,256]{3,2,0,1:T(8,128)}), f32[2,32,8,256]{3,2,0,1:T(8,128)S(1)}, u32[]{:S(2)}, u32[]{:S(2)}) async-start(f32[2,32,8,256]{3,2,0,1:T(8,128)} %pad_maximum_fusion.3), calls=%async_computation | async-start | bytes 1048576 | tf_op jit(solution)/shard_map/all_to_all | solution.py:57
  28.2 85.7 %copy-start.20 = (f32[8,2048]{1,0:T(8,128)}, f32[8,2048]{1,0:T(8,128)S(1)}, u32[]{:S(2)}) copy-start(f32[8,2048]{1,0:T(8,128)S(1)} %fusion.44) | copy-start | bytes 196612
  196.3 53.7 %copy-start.1 = (f32[32,8,256]{2,1,0:T(8,128)S(1)}, f32[32,8,256]{2,1,0:T(8,128)}, u32[]{:S(2)}) copy-start(f32[32,8,256]{2,1,0:T(8,128)} %param.11) | copy-start | bytes 786436
  196.3 53.7 %copy-start.2 = (f32[32,8,256]{2,1,0:T(8,128)S(1)}, f32[32,8,256]{2,1,0:T(8,128)}, u32[]{:S(2)}) copy-start(f32[32,8,256]{2,1,0:T(8,128)} %param.10) | copy-start | bytes 786436
  202.1 50.2 %copy-start.4 = (f32[32]{0:T(128)S(1)}, f32[32]{0:T(128)}, u32[]{:S(2)}) copy-start(f32[32]{0:T(128)} %param.16) | copy-start | bytes 388
  214.4 57.3 %copy-start = (f32[32,8,256]{2,1,0:T(8,128)S(1)}, f32[32,8,256]{2,1,0:T(8,128)}, u32[]{:S(2)}) copy-start(f32[32,8,256]{2,1,0:T(8,128)} %param.17) | copy-start | bytes 786436
  214.4 57.6 %copy-start.6 = (f32[32,8,256]{2,1,0:T(8,128)S(1)}, f32[32,8,256]{2,1,0:T(8,128)}, u32[]{:S(2)}) copy-start(f32[32,8,256]{2,1,0:T(8,128)} %param.12) | copy-start | bytes 786436
  214.4 13.3 %all-to-all-start.1 = ((f32[8,1,16384]{2,1,0:T(1,128)}), f32[8,1,16384]{2,1,0:T(1,128)S(1)}, u32[]{:S(2)}, u32[]{:S(2)}) async-start(f32[8,1,16384]{2,1,0:T(1,128)} %reshape.77), calls=%async_computation.1 | async-start | bytes 1048576 | tf_op jit(solution)/shard_map/all_to_all | solution.py:61
  218.1 74.3 %copy-start.23 = (pred[8]{0:T(512)(128)(4,1)}, pred[8]{0:T(512)(128)(4,1)S(1)}, u32[]{:S(2)}) copy-start(pred[8]{0:T(512)(128)(4,1)S(1)} %dynamic-slice_compare_fusion) | copy-start | bytes 28
  250.2 4.3 collective-permute-start.5
  250.6 6.1 %collective-permute-start.4 = (f32[2,32,1,256]{3,2,1,0:T(1,128)S(1)}, f32[2,32,1,256]{3,2,1,0:T(1,128)S(1)}, u32[]{:S(2)}, u32[]{:S(2)}) collective-permute-start(f32[2,32,1,256]{3,2,1,0:T(1,128)S(1)} %get-tuple-element.206), channel_id=1, source_target_pairs={{0,8},{8,16},{16,24},{24,0},{1,9},{9,17},{17,25},{25,1},{2,10},{10... | collective-permute-start | bytes 196616 | tf_op jit(solution)/shard_map/ppermute | solution.py:16
  257.2 11.9 %collective-permute-start.7 = (f32[2,32,10,1]{3,2,1,0:T(8,128)S(1)}, f32[2,32,10,1]{3,2,1,0:T(8,128)S(1)}, u32[]{:S(2)}, u32[]{:S(2)}) collective-permute-start(f32[2,32,10,1]{3,2,1,0:T(8,128)S(1)} %get-tuple-element.195), channel_id=1, source_target_pairs={{1,0},{2,1},{3,2},{4,3},{5,4},{6,5},{7,6},{0,7},{9,8},{10,9},{11,1... | collective-permute-start | bytes 7688 | tf_op jit(solution)/shard_map/ppermute | solution.py:19
  257.2 13.3 %collective-permute-start.6 = (f32[2,32,10,1]{3,2,1,0:T(8,128)S(1)}, f32[2,32,10,1]{3,2,1,0:T(8,128)S(1)}, u32[]{:S(2)}, u32[]{:S(2)}) collective-permute-start(f32[2,32,10,1]{3,2,1,0:T(8,128)S(1)} %get-tuple-element.194), channel_id=1, source_target_pairs={{0,1},{1,2},{2,3},{3,4},{4,5},{5,6},{6,7},{7,0},{8,9},{9,10},{10,1... | collective-permute-start | bytes 7688 | tf_op jit(solution)/shard_map/ppermute | solution.py:16
  295.1 4.3 collective-permute-start.9
  295.5 5.7 collective-permute-start.8
  301.5 6.1 %collective-permute-start.11 = (f32[32,10,1]{2,1,0:T(8,128)S(1)}, f32[32,10,1]{2,1,0:T(8,128)S(1)}, u32[]{:S(2)}, u32[]{:S(2)}) collective-permute-start(f32[32,10,1]{2,1,0:T(8,128)S(1)} %get-tuple-element.205), channel_id=1, source_target_pairs={{1,0},{2,1},{3,2},{4,3},{5,4},{6,5},{7,6},{0,7},{9,8},{10,9},{11,1... | collective-permute-start | bytes 3848 | tf_op jit(solution)/shard_map/ppermute | solution.py:19
  301.5 8.3 %collective-permute-start.10 = (f32[32,10,1]{2,1,0:T(8,128)S(1)}, f32[32,10,1]{2,1,0:T(8,128)S(1)}, u32[]{:S(2)}, u32[]{:S(2)}) collective-permute-start(f32[32,10,1]{2,1,0:T(8,128)S(1)} %get-tuple-element.204), channel_id=1, source_target_pairs={{0,1},{1,2},{2,3},{3,4},{4,5},{5,6},{6,7},{7,0},{8,9},{9,10},{10,1... | collective-permute-start | bytes 3848 | tf_op jit(solution)/shard_map/ppermute | solution.py:16
  325.0 77.2 %copy-start.22 = (s32[2048]{0:T(1024)S(1)}, s32[2048]{0:T(1024)}, u32[]{:S(2)}) copy-start(s32[2048]{0:T(1024)} %copy-done.21) | copy-start | bytes 24580
  325.0 77.2 %copy-start.25 = (pred[2048]{0:T(1024)(128)(4,1)S(1)}, pred[2048]{0:T(1024)(128)(4,1)}, u32[]{:S(2)}) copy-start(pred[2048]{0:T(1024)(128)(4,1)} %copy-done.24) | copy-start | bytes 6148
  538.4 5.0 collective-permute-start.13
  538.7 6.1 %collective-permute-start.12 = (f32[2,32,1,256]{3,2,0,1:T(1,128)S(1)}, f32[2,32,1,256]{3,2,0,1:T(1,128)S(1)}, u32[]{:S(2)}, u32[]{:S(2)}) collective-permute-start(f32[2,32,1,256]{3,2,0,1:T(1,128)S(1)} %get-tuple-element.200), channel_id=1, source_target_pairs={{0,8},{8,16},{16,24},{24,0},{1,9},{9,17},{17,25},{25,1},{2,10},{10... | collective-permute-start | bytes 196616 | tf_op jit(solution)/shard_map/ppermute | solution.py:16
  545.2 12.1 %collective-permute-start.15 = (f32[2,32,10,1]{3,2,0,1:T(8,128)S(1)}, f32[2,32,10,1]{3,2,0,1:T(8,128)S(1)}, u32[]{:S(2)}, u32[]{:S(2)}) collective-permute-start(f32[2,32,10,1]{3,2,0,1:T(8,128)S(1)} %get-tuple-element.193), channel_id=1, source_target_pairs={{1,0},{2,1},{3,2},{4,3},{5,4},{6,5},{7,6},{0,7},{9,8},{10,9},{11,1... | collective-permute-start | bytes 7688 | tf_op jit(solution)/shard_map/ppermute | solution.py:19
  545.3 13.3 %collective-permute-start.14 = (f32[2,32,10,1]{3,2,0,1:T(8,128)S(1)}, f32[2,32,10,1]{3,2,0,1:T(8,128)S(1)}, u32[]{:S(2)}, u32[]{:S(2)}) collective-permute-start(f32[2,32,10,1]{3,2,0,1:T(8,128)S(1)} %get-tuple-element.192), channel_id=1, source_target_pairs={{0,1},{1,2},{2,3},{3,4},{4,5},{5,6},{6,7},{7,0},{8,9},{9,10},{10,1... | collective-permute-start | bytes 7688 | tf_op jit(solution)/shard_map/ppermute | solution.py:16
  (19 other events, 467.6 us)
where the time goes:
time: 589 us; the launch traced here: 585 us
  matrix products  318 us (54%)
  local copies, waits for them, and re-layouts  82 us (14%)
  waiting for transfers between devices  74.9 us (13%)
  other arithmetic  61.9 us (11%)
  blocking collectives  25.1 us (4%)
  starting transfers between devices  21.6 us (4%)
    dot_general x2, matrix products, transform_band(): jnp.einsum('vetc,cj->vetj', scaled, inverse, precision=lax.Precision.HIGH...  165 us
    dot_general x2, matrix products, transform_band(): jnp.einsum('vetj,jc->vetc', circles, forward, precision=lax.Precision.HIG...  153 us
    unnamed x129, local copies, waits for them, and re-layouts  50.8 us
    div x2, other arithmetic, column_solve(): prev_value = (rhs + below * prev_value) / pivot  41.1 us
    ppermute x8, waiting for transfers between devices, extended(): lax.ppermute(lax.slice_in_dim(block, 0, width, axis=dim), axis, backward)  39.1 us
    ppermute x8, waiting for transfers between devices, extended(): lax.ppermute(lax.slice_in_dim(block, block.shape[dim] - width, None, axis...  16.8 us
    all_to_all x3, local copies, waits for them, and re-layouts, transform_band(): lax.all_to_all(damped, 'lon', split_axis=3, concat_axis=1, tiled=True)  13.9 us
    all_to_all x1, blocking collectives, transform_band(): lax.all_to_all(damped, 'lon', split_axis=3, concat_axis=1, tiled=True)  12.8 us
  transfers between devices with their start and end apart: 18, of which 17 were waited for; matrix products, arithmetic and copies ran while one was open for 1% of the time, Pallas kernels for 0%

commit v1 on v0

--- a/solution.py
+++ b/solution.py
@@ -5,6 +5,12 @@
 from jax.sharding import PartitionSpec as P
 
 SUBSTEPS = 2
+
+
+def stacked_exchange(x, axis, split, join):
+    shards = jnp.split(x, lax.axis_size(axis), axis=split)
+    incoming = lax.all_to_all(jnp.stack(shards), axis, 0, 0)
+    return jnp.concatenate(incoming, axis=join)
 
 
 def extended(block, sides, width):
@@ -58,7 +64,7 @@
     spectra = jnp.einsum("vetj,jc->vetc", circles, forward, precision=lax.Precision.HIGHEST)
     scaled = spectra * damping(wave_row, limits)
     damped = jnp.einsum("vetc,cj->vetj", scaled, inverse, precision=lax.Precision.HIGHEST)
-    return lax.all_to_all(damped, "lon", split_axis=3, concat_axis=1, tiled=True)
+    return stacked_exchange(damped, "lon", 3, 1)
 
 
 def filtered_increments(increments, own_flags, own_limits, forward, inverse, wave_row):

time: 589 us -> 511 us (0.87)
  local copies, waits for them, and re-layouts: 82 us -> 12.5 us
  other arithmetic: 61.9 us -> 53.9 us
    unnamed x129 -> x215, local copies, waits for them, and re-layouts: 50.8 us -> 4.98 us
    all_to_all x3 -> x0, local copies, waits for them, and re-layouts: 13.9 us -> none  [transform_band(): lax.all_to_all(damped, 'lon', split_axis=3, concat_axis=1, tiled=True)]
    dot_general x2 -> x0, local copies, waits for them, and re-layouts: 11.5 us -> none  [transform_band(): jnp.einsum('vetc,cj->vetj', scaled, inverse, precision=lax.Precision.HIGH...]
where the time goes in v1:
time: 511 us; the launch traced here: 507 us
  matrix products  317 us (62%)
  waiting for transfers between devices  75.3 us (15%)
  other arithmetic  53.9 us (11%)
  blocking collectives  24.4 us (5%)
  starting transfers between devices  21.1 us (4%)
  local copies, waits for them, and re-layouts  12.5 us (2%)
    dot_general x2, matrix products, transform_band(): jnp.einsum('vetc,cj->vetj', scaled, inverse, precision=lax.Precision.HIGH...  164 us
    dot_general x2, matrix products, transform_band(): jnp.einsum('vetj,jc->vetc', circles, forward, precision=lax.Precision.HIG...  153 us
    div x2, other arithmetic, column_solve(): prev_value = (rhs + below * prev_value) / pivot  40.4 us
    ppermute x8, waiting for transfers between devices, extended(): lax.ppermute(lax.slice_in_dim(block, 0, width, axis=dim), axis, backward)  39.7 us
    ppermute x8, waiting for transfers between devices, extended(): lax.ppermute(lax.slice_in_dim(block, block.shape[dim] - width, None, axis...  16.5 us
    all_to_all x1, blocking collectives, transform_band(): lax.all_to_all(block, 'lon', split_axis=1, concat_axis=3, tiled=True)  12.3 us
    all_to_all x1, blocking collectives, stacked_exchange(): incoming = lax.all_to_all(jnp.stack(shards), axis, 0, 0)  12.1 us
  transfers between devices with their start and end apart: 18, of which 17 were waited for; matrix products, arithmetic and copies ran while one was open for 1% of the time, Pallas kernels for 0%

profile of v1, /device:TPU:0, one launch (start us, length us, event | category | flops | bytes accessed | tf_op | source)
XLA Modules:
  0.0 507.3 jit_solution(1169410655252019513)
XLA Ops:
  1.8 5.1 %collective-permute-start.1 = (f32[32,1,256]{2,1,0:T(1,128)S(1)}, f32[32,1,256]{2,1,0:T(1,128)S(1)}, u32[]{:S(2)}, u32[]{:S(2)}) collective-permute-start(f32[32,1,256]{2,1,0:T(1,128)S(1)} %get-tuple-element.213), channel_id=1, source_target_pairs={{8,0},{16,8},{24,16},{0,24},{9,1},{17,9},{25,17},{1,25},{10,2},{18... | collective-permute-start | bytes 98312 | tf_op jit(solution)/shard_map/ppermute | solution.py:25
  7.0 2.1 iota_select_fusion
  9.1 3.5 collective-permute-done
  13.5 6.1 %collective-permute-done.3 = f32[32,10,1]{2,1,0:T(8,128)S(1)} collective-permute-done((f32[32,10,1]{2,1,0:T(8,128)S(1)}, f32[32,10,1]{2,1,0:T(8,128)S(1)}, u32[]{:S(2)}, u32[]{:S(2)}) %collective-permute-start.3) | collective-permute-done | bytes 1312 | tf_op jit(solution)/shard_map/ppermute | solution.py:25
  19.5 3.0 collective-permute-done.2
  24.3 3.7 all-to-all-start
  28.1 9.5 %all-to-all-done = f32[2,32,8,256]{3,2,0,1:T(8,128)S(1)} async-done(((f32[2,32,8,256]{3,2,0,1:T(8,128)}), f32[2,32,8,256]{3,2,0,1:T(8,128)S(1)}, u32[]{:S(2)}, u32[]{:S(2)}) %all-to-all-start) | async-done | bytes 524320 | tf_op jit(solution)/shard_map/all_to_all | solution.py:63
  38.0 75.8 %fusion.15 = f32[2,4,8,2048]{3,2,1,0:T(8,128)S(1)} fusion(f32[2,4,8,2048]{3,2,1,0:T(8,128)S(1)} %all_to_all.35, s32[2048]{0:T(1024)S(1)} %iota_add_fusion, pred[2048]{0:T(1024)(128)(4,1)S(1)} %iota_compare_fusion, f32[8,2048]{1,0:T(8,128)S(1)} %fusion.43), kind=kOutput, calls=%fused_computation.21 | convolution fusion | flops 3288465408 | bytes 1124352 | tf_op jit(solution)/shard_map/vetj,jc->vetc/dot_general | solution.py:64
  113.9 82.3 %fusion.5 = f32[2,4,8,2048]{3,2,1,0:T(8,128)S(1)} fusion(f32[2,4,8,2048]{3,2,1,0:T(8,128)S(1)} %fusion.15, s32[2048]{0:T(1024)S(1)} %iota_add_fusion, pred[2048]{0:T(1024)(128)(4,1)S(1)} %iota_compare_fusion), kind=kOutput, calls=%fused_computation.8 | convolution fusion | flops 3317694464 | bytes 1058816 | tf_op jit(solution)/shard_map/vetc,cj->vetj/dot_general | solution.py:66
  201.2 3.5 all-to-all-start.1
  204.8 9.6 %all-to-all-done.1 = f32[8,2,4,8,256]{4,3,2,1,0:T(8,128)S(1)} async-done(((f32[8,2,4,8,256]{4,3,2,1,0:T(8,128)}), f32[8,2,4,8,256]{4,3,2,1,0:T(8,128)S(1)}, u32[]{:S(2)}, u32[]{:S(2)}) %all-to-all-start.1) | async-done | bytes 524320 | tf_op jit(solution)/shard_map/all_to_all | solution.py:12
  215.1 1.7 collective-permute-start.4
  217.5 1.5 collective-permute-done.5
  219.0 2.1 collective-permute-done.4
  222.9 10.7 %collective-permute-done.7 = f32[2,32,10,1]{3,2,1,0:T(8,128)S(1)} collective-permute-done((f32[2,32,10,1]{3,2,1,0:T(8,128)S(1)}, f32[2,32,10,1]{3,2,1,0:T(8,128)S(1)}, u32[]{:S(2)}, u32[]{:S(2)}) %collective-permute-start.7) | collective-permute-done | bytes 2592 | tf_op jit(solution)/shard_map/ppermute | solution.py:25
  236.3 20.2 %add_divide_fusion.32 = (f32[1,8,256]{2,1,0:T(8,128)S(1)}, f32[1,8,256]{2,1,0:T(8,128)S(1)}, f32[1,8,256]{2,1,0:T(8,128)S(1)}, f32[1,8,256]{2,1,0:T(8,128)S(1)},...) fusion(f32[32,8,256]{2,1,0:T(8,128)S(1)} %copy-done.6, ...), kind=kLoop, calls=%fused_computation.341 | loop fusion | flops 882688 | bytes 1523836 | tf_op jit(solution)/shard_map/div | solution.py:94
  256.5 2.1 constant_dynamic-update-slice_fusion.70
  259.6 1.6 collective-permute-start.8
  261.3 2.2 collective-permute-done.9
  263.5 1.8 collective-permute-done.8
  266.1 5.8 %collective-permute-done.11 = f32[32,10,1]{2,1,0:T(8,128)S(1)} collective-permute-done((f32[32,10,1]{2,1,0:T(8,128)S(1)}, f32[32,10,1]{2,1,0:T(8,128)S(1)}, u32[]{:S(2)}, u32[]{:S(2)}) %collective-permute-start.11) | collective-permute-done | bytes 1312 | tf_op jit(solution)/shard_map/ppermute | solution.py:25
  271.9 2.0 collective-permute-done.10
  274.9 12.3 %all_to_all.46 = f32[2,32,8,256]{3,2,0,1:T(8,128)S(1)} all-to-all(f32[2,32,8,256]{3,2,0,1:T(8,128)S(1)} %copy.21), channel_id=1, replica_groups=mesh['lat'=4,'lon'=8] {'lon'}, dimensions={1} | all-to-all | bytes 1048576 | tf_op jit(solution)/shard_map/all_to_all | solution.py:63
  288.4 77.2 %fusion.18 = f32[2,4,8,2048]{3,2,1,0:T(8,128)S(1)} fusion(f32[2,4,8,2048]{3,2,1,0:T(8,128)} %all_to_all.40, s32[2048]{0:T(1024)} %copy-done.61, pred[2048]{0:T(1024)(128)(4,1)} %copy-done.63, f32[8,2048]{1,0:T(8,128)} %copy-done.33), kind=kOutput, calls=%fused_computation.22 | convolution fusion | flops 3288465408 | bytes 1124352 | tf_op jit(solution)/shard_map/vetj,jc->vetc/dot_general | solution.py:64
  366.1 82.2 %fusion.3 = f32[2,4,8,2048]{3,2,1,0:T(8,128)S(1)} fusion(f32[2,4,8,2048]{3,2,1,0:T(8,128)S(1)} %fusion.18, s32[2048]{0:T(1024)S(1)} %copy-done.62, pred[2048]{0:T(1024)(128)(4,1)S(1)} %copy-done.64), kind=kOutput, calls=%fused_computation.6 | convolution fusion | flops 3317694464 | bytes 1058816 | tf_op jit(solution)/shard_map/vetc,cj->vetj/dot_general | solution.py:66
  448.4 12.1 %all_to_all.47 = f32[8,2,4,8,256]{4,3,2,1,0:T(8,128)S(1)} all-to-all(f32[8,2,4,8,256]{4,3,2,1,0:T(8,128)S(1)} %constant_dynamic-update-slice_fusion.71), channel_id=1, replica_groups=mesh['lat'=4,'lon'=8] {'lon'}, dimensions={0} | all-to-all | bytes 1048576 | tf_op jit(solution)/shard_map/all_to_all | solution.py:12
  462.0 1.6 collective-permute-start.12
  463.5 2.9 collective-permute-done.13
  466.5 1.6 collective-permute-done.12
  470.0 10.5 %collective-permute-done.15 = f32[2,32,10,1]{3,2,1,0:T(8,128)S(1)} collective-permute-done((f32[2,32,10,1]{3,2,1,0:T(8,128)S(1)}, f32[2,32,10,1]{3,2,1,0:T(8,128)S(1)}, u32[]{:S(2)}, u32[]{:S(2)}) %collective-permute-start.15) | collective-permute-done | bytes 2592 | tf_op jit(solution)/shard_map/ppermute | solution.py:25
  481.8 1.8 maximum_select_fusion.1
  484.9 20.2 %add_divide_fusion.1 = (f32[1,8,256]{2,1,0:T(8,128)S(1)}, f32[1,8,256]{2,1,0:T(8,128)S(1)}, f32[1,8,256]{2,1,0:T(8,128)S(1)}, f32[1,8,256]{2,1,0:T(8,128)S(1)}, ...) fusion(f32[1,8,256]{2,1,0:T(8,128)S(1)} %get-tuple-element.102,, ...), kind=kLoop, calls=%fused_computation.276 | loop fusion | flops 452608 | bytes 1269884 | tf_op jit(solution)/shard_map/div | solution.py:94
  (284 shorter events, 26.4 us)
Async XLA Ops:
  1.8 7.3 %collective-permute-start.1 = (f32[32,1,256]{2,1,0:T(1,128)S(1)}, f32[32,1,256]{2,1,0:T(1,128)S(1)}, u32[]{:S(2)}, u32[]{:S(2)}) collective-permute-start(f32[32,1,256]{2,1,0:T(1,128)S(1)} %get-tuple-element.213), channel_id=1, source_target_pairs={{8,0},{16,8},{24,16},{0,24},{9,1},{17,9},{25,17},{1,25},{10,2},{18... | collective-permute-start | bytes 98312 | tf_op jit(solution)/shard_map/ppermute | solution.py:25
  6.9 5.7 %collective-permute-start = (f32[32,1,256]{2,1,0:T(1,128)S(1)}, f32[32,1,256]{2,1,0:T(1,128)S(1)}, u32[]{:S(2)}, u32[]{:S(2)}) collective-permute-start(f32[32,1,256]{2,1,0:T(1,128)S(1)} %get-tuple-element.212), channel_id=1, source_target_pairs={{0,8},{8,16},{16,24},{24,0},{1,9},{9,17},{17,25},{25,1},{2,10},{10... | collective-permute-start | bytes 98312 | tf_op jit(solution)/shard_map/ppermute | solution.py:22
  12.9 6.7 %collective-permute-start.3 = (f32[32,10,1]{2,1,0:T(8,128)S(1)}, f32[32,10,1]{2,1,0:T(8,128)S(1)}, u32[]{:S(2)}, u32[]{:S(2)}) collective-permute-start(f32[32,10,1]{2,1,0:T(8,128)S(1)} %get-tuple-element.209), channel_id=1, source_target_pairs={{1,0},{2,1},{3,2},{4,3},{5,4},{6,5},{7,6},{0,7},{9,8},{10,9},{11,1... | collective-permute-start | bytes 3848 | tf_op jit(solution)/shard_map/ppermute | solution.py:25
  13.4 9.2 %collective-permute-start.2 = (f32[32,10,1]{2,1,0:T(8,128)S(1)}, f32[32,10,1]{2,1,0:T(8,128)S(1)}, u32[]{:S(2)}, u32[]{:S(2)}) collective-permute-start(f32[32,10,1]{2,1,0:T(8,128)S(1)} %get-tuple-element.208), channel_id=1, source_target_pairs={{0,1},{1,2},{2,3},{3,4},{4,5},{5,6},{6,7},{7,0},{8,9},{9,10},{10,1... | collective-permute-start | bytes 3848 | tf_op jit(solution)/shard_map/ppermute | solution.py:22
  13.4 260.5 %copy-start.65 = (pred[10]{0:T(512)(128)(4,1)}, pred[10]{0:T(512)(128)(4,1)S(1)}, u32[]{:S(2)}) copy-start(pred[10]{0:T(512)(128)(4,1)S(1)} %and_or_fusion) | copy-start | bytes 34
  24.3 13.3 %all-to-all-start = ((f32[2,32,8,256]{3,2,0,1:T(8,128)}), f32[2,32,8,256]{3,2,0,1:T(8,128)S(1)}, u32[]{:S(2)}, u32[]{:S(2)}) async-start(f32[2,32,8,256]{3,2,0,1:T(8,128)} %copy.18), calls=%async_computation | async-start | bytes 1048576 | tf_op jit(solution)/shard_map/all_to_all | solution.py:63
  113.9 122.1 %copy-start = (f32[32,8,256]{2,1,0:T(8,128)S(1)}, f32[32,8,256]{2,1,0:T(8,128)}, u32[]{:S(2)}) copy-start(f32[32,8,256]{2,1,0:T(8,128)} %param.17) | copy-start | bytes 786436
  113.9 122.4 %copy-start.6 = (f32[32,8,256]{2,1,0:T(8,128)S(1)}, f32[32,8,256]{2,1,0:T(8,128)}, u32[]{:S(2)}) copy-start(f32[32,8,256]{2,1,0:T(8,128)} %param.12) | copy-start | bytes 786436
  201.2 13.1 %all-to-all-start.1 = ((f32[8,2,4,8,256]{4,3,2,1,0:T(8,128)}), f32[8,2,4,8,256]{4,3,2,1,0:T(8,128)S(1)}, u32[]{:S(2)}, u32[]{:S(2)}) async-start(f32[8,2,4,8,256]{4,3,2,1,0:T(8,128)} %constant_dynamic-update-slice_fusion), calls=%async_computation.1 | async-start | bytes 1048576 | tf_op jit(solution)/shard_map/all_to_all | solution.py:12
  214.7 4.3 collective-permute-start.5
  215.1 6.1 %collective-permute-start.4 = (f32[2,32,1,256]{3,2,1,0:T(1,128)S(1)}, f32[2,32,1,256]{3,2,1,0:T(1,128)S(1)}, u32[]{:S(2)}, u32[]{:S(2)}) collective-permute-start(f32[2,32,1,256]{3,2,1,0:T(1,128)S(1)} %get-tuple-element.206), channel_id=1, source_target_pairs={{0,8},{8,16},{16,24},{24,0},{1,9},{9,17},{17,25},{25,1},{2,10},{10... | collective-permute-start | bytes 196616 | tf_op jit(solution)/shard_map/ppermute | solution.py:22
  221.5 12.2 %collective-permute-start.7 = (f32[2,32,10,1]{3,2,1,0:T(8,128)S(1)}, f32[2,32,10,1]{3,2,1,0:T(8,128)S(1)}, u32[]{:S(2)}, u32[]{:S(2)}) collective-permute-start(f32[2,32,10,1]{3,2,1,0:T(8,128)S(1)} %get-tuple-element.195), channel_id=1, source_target_pairs={{1,0},{2,1},{3,2},{4,3},{5,4},{6,5},{7,6},{0,7},{9,8},{10,9},{11,1... | collective-permute-start | bytes 7688 | tf_op jit(solution)/shard_map/ppermute | solution.py:25
  221.6 13.3 %collective-permute-start.6 = (f32[2,32,10,1]{3,2,1,0:T(8,128)S(1)}, f32[2,32,10,1]{3,2,1,0:T(8,128)S(1)}, u32[]{:S(2)}, u32[]{:S(2)}) collective-permute-start(f32[2,32,10,1]{3,2,1,0:T(8,128)S(1)} %get-tuple-element.194), channel_id=1, source_target_pairs={{0,1},{1,2},{2,3},{3,4},{4,5},{5,6},{6,7},{7,0},{8,9},{9,10},{10,1... | collective-permute-start | bytes 7688 | tf_op jit(solution)/shard_map/ppermute | solution.py:22
  259.2 4.3 collective-permute-start.9
  259.6 5.7 %collective-permute-start.8 = (f32[32,1,256]{2,1,0:T(1,128)S(1)}, f32[32,1,256]{2,1,0:T(1,128)S(1)}, u32[]{:S(2)}, u32[]{:S(2)}) collective-permute-start(f32[32,1,256]{2,1,0:T(1,128)S(1)} %get-tuple-element.210), channel_id=1, source_target_pairs={{0,8},{8,16},{16,24},{24,0},{1,9},{9,17},{17,25},{25,1},{2,10},{10... | collective-permute-start | bytes 98312 | tf_op jit(solution)/shard_map/ppermute | solution.py:22
  265.6 6.3 %collective-permute-start.11 = (f32[32,10,1]{2,1,0:T(8,128)S(1)}, f32[32,10,1]{2,1,0:T(8,128)S(1)}, u32[]{:S(2)}, u32[]{:S(2)}) collective-permute-start(f32[32,10,1]{2,1,0:T(8,128)S(1)} %get-tuple-element.205), channel_id=1, source_target_pairs={{1,0},{2,1},{3,2},{4,3},{5,4},{6,5},{7,6},{0,7},{9,8},{10,9},{11,1... | collective-permute-start | bytes 3848 | tf_op jit(solution)/shard_map/ppermute | solution.py:25
  265.7 8.2 %collective-permute-start.10 = (f32[32,10,1]{2,1,0:T(8,128)S(1)}, f32[32,10,1]{2,1,0:T(8,128)S(1)}, u32[]{:S(2)}, u32[]{:S(2)}) collective-permute-start(f32[32,10,1]{2,1,0:T(8,128)S(1)} %get-tuple-element.204), channel_id=1, source_target_pairs={{0,1},{1,2},{2,3},{3,4},{4,5},{5,6},{6,7},{7,0},{8,9},{9,10},{10,1... | collective-permute-start | bytes 3848 | tf_op jit(solution)/shard_map/ppermute | solution.py:22
  365.7 118.9 %copy-start.8 = (f32[1,8,256]{2,1,0:T(8,128)S(1)}, f32[1,8,256]{2,1,0:T(8,128)}, u32[]{:S(2)}) copy-start(f32[1,8,256]{2,1,0:T(8,128)} %copy-done.7) | copy-start | bytes 24580
  365.7 118.9 %copy-start.10 = (f32[1,8,256]{2,1,0:T(8,128)S(1)}, f32[1,8,256]{2,1,0:T(8,128)}, u32[]{:S(2)}) copy-start(f32[1,8,256]{2,1,0:T(8,128)} %copy-done.9) | copy-start | bytes 24580
  365.7 118.9 %copy-start.12 = (f32[1,8,256]{2,1,0:T(8,128)S(1)}, f32[1,8,256]{2,1,0:T(8,128)}, u32[]{:S(2)}) copy-start(f32[1,8,256]{2,1,0:T(8,128)} %copy-done.11) | copy-start | bytes 24580
  365.7 118.9 %copy-start.14 = (f32[1,8,256]{2,1,0:T(8,128)S(1)}, f32[1,8,256]{2,1,0:T(8,128)}, u32[]{:S(2)}) copy-start(f32[1,8,256]{2,1,0:T(8,128)} %copy-done.13) | copy-start | bytes 24580
  365.7 118.9 %copy-start.16 = (f32[1,8,256]{2,1,0:T(8,128)S(1)}, f32[1,8,256]{2,1,0:T(8,128)}, u32[]{:S(2)}) copy-start(f32[1,8,256]{2,1,0:T(8,128)} %copy-done.15) | copy-start | bytes 24580
  365.7 118.9 %copy-start.18 = (f32[1,8,256]{2,1,0:T(8,128)S(1)}, f32[1,8,256]{2,1,0:T(8,128)}, u32[]{:S(2)}) copy-start(f32[1,8,256]{2,1,0:T(8,128)} %copy-done.17) | copy-start | bytes 24580
  365.7 118.9 %copy-start.20 = (f32[1,8,256]{2,1,0:T(8,128)S(1)}, f32[1,8,256]{2,1,0:T(8,128)}, u32[]{:S(2)}) copy-start(f32[1,8,256]{2,1,0:T(8,128)} %copy-done.19) | copy-start | bytes 24580
  365.7 118.9 %copy-start.22 = (f32[1,8,256]{2,1,0:T(8,128)S(1)}, f32[1,8,256]{2,1,0:T(8,128)}, u32[]{:S(2)}) copy-start(f32[1,8,256]{2,1,0:T(8,128)} %copy-done.21) | copy-start | bytes 24580
  365.8 118.9 %copy-start.24 = (f32[1,8,256]{2,1,0:T(8,128)S(1)}, f32[1,8,256]{2,1,0:T(8,128)}, u32[]{:S(2)}) copy-start(f32[1,8,256]{2,1,0:T(8,128)} %copy-done.23) | copy-start | bytes 24580
  365.8 118.9 %copy-start.26 = (f32[1,8,256]{2,1,0:T(8,128)S(1)}, f32[1,8,256]{2,1,0:T(8,128)}, u32[]{:S(2)}) copy-start(f32[1,8,256]{2,1,0:T(8,128)} %copy-done.25) | copy-start | bytes 24580
  365.8 118.9 %copy-start.28 = (f32[1,8,256]{2,1,0:T(8,128)S(1)}, f32[1,8,256]{2,1,0:T(8,128)}, u32[]{:S(2)}) copy-start(f32[1,8,256]{2,1,0:T(8,128)} %copy-done.27) | copy-start | bytes 24580
  461.4 5.0 collective-permute-start.13
  462.0 6.1 %collective-permute-start.12 = (f32[2,32,1,256]{3,2,1,0:T(1,128)S(1)}, f32[2,32,1,256]{3,2,1,0:T(1,128)S(1)}, u32[]{:S(2)}, u32[]{:S(2)}) collective-permute-start(f32[2,32,1,256]{3,2,1,0:T(1,128)S(1)} %get-tuple-element.200), channel_id=1, source_target_pairs={{0,8},{8,16},{16,24},{24,0},{1,9},{9,17},{17,25},{25,1},{2,10},{10... | collective-permute-start | bytes 196616 | tf_op jit(solution)/shard_map/ppermute | solution.py:22
  468.4 12.1 %collective-permute-start.15 = (f32[2,32,10,1]{3,2,1,0:T(8,128)S(1)}, f32[2,32,10,1]{3,2,1,0:T(8,128)S(1)}, u32[]{:S(2)}, u32[]{:S(2)}) collective-permute-start(f32[2,32,10,1]{3,2,1,0:T(8,128)S(1)} %get-tuple-element.193), channel_id=1, source_target_pairs={{1,0},{2,1},{3,2},{4,3},{5,4},{6,5},{7,6},{0,7},{9,8},{10,9},{11,1... | collective-permute-start | bytes 7688 | tf_op jit(solution)/shard_map/ppermute | solution.py:25
  468.5 13.3 %collective-permute-start.14 = (f32[2,32,10,1]{3,2,1,0:T(8,128)S(1)}, f32[2,32,10,1]{3,2,1,0:T(8,128)S(1)}, u32[]{:S(2)}, u32[]{:S(2)}) collective-permute-start(f32[2,32,10,1]{3,2,1,0:T(8,128)S(1)} %get-tuple-element.192), channel_id=1, source_target_pairs={{0,1},{1,2},{2,3},{3,4},{4,5},{5,6},{6,7},{7,0},{8,9},{9,10},{10,1... | collective-permute-start | bytes 7688 | tf_op jit(solution)/shard_map/ppermute | solution.py:22
  (57 other events, 4585.3 us)
